TPU v7x, 128 devices: a whole 4x4x4 slice. The times are simulated.
128 devices in a mesh: dp: 2 (over core), ep: 64 (over x, y, z).
Axes of the slice: x: 4, y: 4, z: 4, core: 2. Of those that a mesh axis runs over, the one named last changes fastest.
Arguments:
- x: bfloat16 [2, 64, 256, 2048], P('dp', 'ep'), parts along dimension 0
- expert: int32 [2, 64, 256, 8], P('dp', 'ep'), parts along dimension 0
- slot: int32 [2, 64, 256, 8], P('dp', 'ep'), parts along dimension 0
- gate: float32 [2, 64, 256, 8], P('dp', 'ep'), parts along dimension 0
- w_gate: bfloat16 [128, 2048, 1536], P('ep')
- w_up: bfloat16 [128, 2048, 1536], P('ep')
- w_down: bfloat16 [128, 1536, 2048], P('ep')
Outputs:
- y: bfloat16 [2, 64, 256, 2048], P('dp', 'ep'), parts along dimension 0
There are 2 independent parts. A program takes and returns all parts, laid end to end along the dimension named above; an argument that names none is the same for every part.
All inputs are finite; a program needn't handle non-finite values.
Results may differ from a plain program's by a relative error of at most 0.009.
Values are sent between devices in bfloat16 or wider.
A program may use at most 1.5 GiB of HBM per device.

v0:
```python
import jax
import jax.numpy as jnp
from jax import lax
from jax.sharding import NamedSharding, PartitionSpec as P


def einsum(form, a, b):
    return jnp.einsum(form, a.astype(jnp.float32), b.astype(jnp.float32))


def solution(mesh):
    def placed(v, *spec):
        return lax.with_sharding_constraint(v, NamedSharding(mesh, P(*spec)))

    def step(x, expert, slot, gate, w_gate, w_up, w_down):
        experts, (tokens, top) = w_gate.shape[0], expert.shape[2:]
        slots = 5 * tokens * top // (4 * experts)
        to_expert = jax.nn.one_hot(expert, experts, dtype=jnp.bfloat16)
        to_slot = jax.nn.one_hot(slot, slots, dtype=jnp.bfloat16)
        weighted = to_expert * gate[..., None].astype(jnp.bfloat16)
        dispatch = einsum("abtke,abtkc->abtec", to_expert, to_slot).astype(jnp.bfloat16)
        combine = einsum("abtke,abtkc->abtec", weighted, to_slot).astype(jnp.bfloat16)
        z = einsum("abtec,abtd->aebcd", dispatch, x).astype(jnp.bfloat16)
        z = placed(z, "dp", None, "ep", None, None)
        z = placed(z, "dp", "ep", None, None, None)
        h = jax.nn.silu(einsum("aebcd,edf->aebcf", z, w_gate))
        h = (h * einsum("aebcd,edf->aebcf", z, w_up)).astype(jnp.bfloat16)
        out = einsum("aebcf,efd->aebcd", h, w_down).astype(jnp.bfloat16)
        out = placed(out, "dp", "ep", None, None, None)
        out = placed(out, "dp", None, "ep", None, None)
        y = einsum("abtec,aebcd->abtd", combine, out)
        return y.astype(jnp.bfloat16)

    return step
```

profile of v0, /device:TPU:83, one launch (start us, length us, event | category | flops | bytes accessed | tf_op | source)
XLA Modules:
  0.0 558.0 jit_solution(14688473095228885488)
XLA Ops:
  0.0 0.0 copy-start
  0.0 0.9 copy.18
  0.9 0.8 copy.20
  1.7 2.8 convolution_convert_fusion.1
  4.6 0.0 copy-done
  4.6 5.6 convolution_convert_fusion
  10.1 17.3 %reshape.6 = bf16[1,64,2,1,20,2048]{5,2,1,4,3,0:T(2,128)(2,1)} reshape(bf16[128,20,2048]{2,0,1:T(8,128)(2,1)} %convolution_convert_fusion) | data formatting | bytes 20971520 | tf_op jit(solution)/sharding_constraint;jit(solution)/sharding_constraint | solution.py:13
  27.5 11.3 %copy.22 = bf16[1,64,2,1,20,2048]{5,2,4,3,0,1:T(2,128)(2,1)S(1)} copy(bf16[1,64,2,1,20,2048]{5,2,1,4,3,0:T(2,128)(2,1)} %reshape.6) | data formatting | bytes 20971520 | tf_op jit(solution)/sharding_constraint;jit(solution)/sharding_constraint | solution.py:13
  38.7 146.5 %all-to-all.4 = bf16[1,64,2,1,20,2048]{5,2,4,3,0,1:T(2,128)(2,1)} all-to-all(bf16[1,64,2,1,20,2048]{5,2,4,3,0,1:T(2,128)(2,1)S(1)} %copy.22), channel_id=1, replica_groups=mesh['dp'=2,'ep'=64] {'ep'}, dimensions={1} | all-to-all | bytes 20971520 | tf_op jit(solution)/sharding_constraint;jit(solution)/sharding_constraint | solution.py:13
  185.2 51.9 %fusion.6 = f32[2,64,20,1536]{3,1,2,0:T(8,128)} fusion(bf16[2,2048,1536]{2,1,0:T(8,128)(2,1)} %param.5, bf16[1,64,2,1,20,2048]{5,2,4,3,0,1:T(2,128)(2,1)} %all-to-all.4), kind=kOutput, calls=%fused_computation.9 | convolution fusion | flops 16106127360 | bytes 38797312 | tf_op jit(solution)/aebcd,edf->aebcf/dot_general | solution.py:8
  237.1 54.6 %fusion = bf16[1,2,64,20,1536]{4,2,3,1,0:T(8,128)(2,1)} fusion(f32[2,64,20,1536]{3,1,2,0:T(8,128)} %fusion.6, bf16[2,2048,1536]{2,1,0:T(8,128)(2,1)} %param.4, bf16[1,64,2,1,20,2048]{5,2,4,3,0,1:T(2,128)(2,1)} %all-to-all.4), kind=kOutput, calls=%fused_computation.1 | convolution fusion | flops 16129720320 | bytes 46661632 | tf_op jit(solution)/aebcd,edf->aebcf/dot_general | solution.py:8
  291.7 24.0 %convert_bitcast_fusion = bf16[1,2,64,1,20,2048]{5,2,4,1,3,0:T(8,128)(2,1)} fusion(bf16[2,1536,2048]{2,1,0:T(8,128)(2,1)} %param.6, bf16[1,2,64,20,1536]{4,2,3,1,0:T(8,128)(2,1)} %fusion), kind=kOutput, calls=%fused_computation.15 | convolution fusion | flops 16111370240 | bytes 30932992 | tf_op jit(solution)/aebcf,efd->aebcd/dot_general | solution.py:8
  315.7 20.2 %copy.24 = bf16[1,2,64,1,20,2048]{5,1,4,3,0,2:T(2,128)(2,1)} copy(bf16[1,2,64,1,20,2048]{5,2,4,1,3,0:T(8,128)(2,1)} %convert_bitcast_fusion) | data formatting | bytes 20971520 | tf_op jit(solution)/sharding_constraint;jit(solution)/sharding_constraint | solution.py:13
  335.9 0.0 copy-start.2
  335.9 17.5 %all-to-all-start.1 = ((bf16[1,2,64,1,20,2048]{5,1,4,3,0,2:T(2,128)(2,1)}), bf16[1,2,64,1,20,2048]{5,1,4,3,0,2:T(2,128)(2,1)}, u32[]{:S(2)}, u32[]{:S(2)}) async-start(bf16[1,2,64,1,20,2048]{5,1,4,3,0,2:T(2,128)(2,1)} %copy.24), calls=%async_computation.1 | async-start | bytes 20971520 | tf_op jit(solution)/sharding_constraint;jit(solution)/sharding_constraint | solution.py:13
  353.4 0.0 copy-done.2
  353.4 0.1 copy.19
  353.5 3.2 convolution_convert_fusion.2
  356.7 168.7 %all-to-all-done.1 = bf16[1,2,64,1,20,2048]{5,1,4,3,0,2:T(2,128)(2,1)} async-done(((bf16[1,2,64,1,20,2048]{5,1,4,3,0,2:T(2,128)(2,1)}), bf16[1,2,64,1,20,2048]{5,1,4,3,0,2:T(2,128)(2,1)}, u32[]{:S(2)}, u32[]{:S(2)}) %all-to-all-start.1) | async-done | bytes 10485792 | tf_op jit(solution)/sharding_constraint;jit(solution)/sharding_constraint | solution.py:13
  525.5 9.5 %copy.25 = bf16[1,64,2,1,20,2048]{5,2,1,4,3,0:T(2,128)(2,1)} copy(bf16[1,64,2,1,20,2048]{5,2,4,3,0,1:T(2,128)(2,1)} %bitcast.21) | data formatting | bytes 20971520 | tf_op jit(solution)/sharding_constraint;jit(solution)/sharding_constraint | solution.py:13
  535.0 0.0 copy-start.1
  535.0 16.1 %reshape.46 = bf16[128,20,2048]{2,0,1:T(8,128)(2,1)} reshape(bf16[1,64,2,1,20,2048]{5,2,1,4,3,0:T(2,128)(2,1)} %copy.25) | data formatting | bytes 20971520
  551.1 6.7 %fusion.22 = bf16[1,1,256,2048]{3,2,1,0:T(8,128)(2,1)} fusion(bf16[128,20,2048]{2,0,1:T(8,128)(2,1)} %reshape.46, bf16[256,128,20]{1,2,0:T(8,128)(2,1)S(1)} %convolution_convert_fusion.2), kind=kOutput, calls=%fused_computation.22 | convolution fusion | flops 2684878848 | bytes 12845056 | tf_op jit(solution)/abtec,aebcd->abtd/dot_general | solution.py:8
  557.8 0.0 copy-done.1
  (1 shorter events, 0.0 us)
Async XLA Ops:
  0.0 4.6 copy-start
  335.9 17.5 %copy-start.2 = (f32[1,1,256,8]{2,3,1,0:T(8,128)S(1)}, f32[1,1,256,8]{2,3,1,0:T(8,128)}, u32[]{:S(2)}) copy-start(f32[1,1,256,8]{2,3,1,0:T(8,128)} %param.1) | copy-start | bytes 24580
  335.9 189.5 %all-to-all-start.1 = ((bf16[1,2,64,1,20,2048]{5,1,4,3,0,2:T(2,128)(2,1)}), bf16[1,2,64,1,20,2048]{5,1,4,3,0,2:T(2,128)(2,1)}, u32[]{:S(2)}, u32[]{:S(2)}) async-start(bf16[1,2,64,1,20,2048]{5,1,4,3,0,2:T(2,128)(2,1)} %copy.24), calls=%async_computation.1 | async-start | bytes 20971520 | tf_op jit(solution)/sharding_constraint;jit(solution)/sharding_constraint | solution.py:13
  535.0 22.8 %copy-start.1 = (bf16[1,1,256,2048]{3,2,1,0:T(8,128)(2,1)S(1)}, bf16[1,1,256,2048]{3,2,1,0:T(8,128)(2,1)}, u32[]{:S(2)}) copy-start(bf16[1,1,256,2048]{3,2,1,0:T(8,128)(2,1)} %param.3) | copy-start | bytes 3145732
where the time goes:
time: 567 us; the launch traced here: 558 us
  waiting for transfers between devices  169 us (30%)
  matrix products  149 us (26%)
  blocking collectives  146 us (26%)
  local copies, waits for them, and re-layouts  76.3 us (13%)
  starting transfers between devices  17.5 us (3%)
    another operation x1, waiting for transfers between devices, placed(): return lax.with_sharding_constraint(v, NamedSharding(mesh, P(*spec)))  169 us
    dot_general x7, matrix products, einsum(): return jnp.einsum(form, a.astype(jnp.float32), b.astype(jnp.float32))  149 us
    another operation x1, blocking collectives, placed(): return lax.with_sharding_constraint(v, NamedSharding(mesh, P(*spec)))  146 us
    another operation x4, local copies, waits for them, and re-layouts, placed(): return lax.with_sharding_constraint(v, NamedSharding(mesh, P(*spec)))  58.3 us
    unnamed x9, local copies, waits for them, and re-layouts  17.9 us
    another operation x1, starting transfers between devices, placed(): return lax.with_sharding_constraint(v, NamedSharding(mesh, P(*spec)))  17.5 us
  transfers between devices with their start and end apart: 1, of which 1 were waited for; matrix products, arithmetic and copies ran while one was open for 1% of the time, Pallas kernels for 0%

commit v1 on v0

v1 whole, which is shorter than its diff:
```python
import functools

import jax
import jax.numpy as jnp
from jax import lax
from jax.experimental import pallas as pl
from jax.experimental.pallas import tpu as pltpu
from jax.sharding import PartitionSpec as P

F32, BF16, I32 = jnp.float32, jnp.bfloat16, jnp.int32
TILE = 256
LANES = 128
VMEM_LIMIT = 60 * 2**20


def iota(shape, dim):
    return lax.broadcasted_iota(I32, shape, dim)


def dot(a, b):
    return jnp.dot(a, b, preferred_element_type=F32)


def pack_kernel(post_ref, x_ref, rows_ref):
    tokens = x_ref.shape[0]
    at = iota((TILE, tokens), 0) + pl.program_id(0) * TILE
    hit = at == post_ref[0:1, :]
    for j in range(1, post_ref.shape[0]):
        hit = hit | (at == post_ref[j : j + 1, :])
    rows = dot(jnp.where(hit, 1.0, 0.0).astype(BF16), x_ref[...])
    rows_ref[...] = rows.reshape(rows_ref.shape).astype(BF16)


def pack(post, x, rows):
    tokens, depth = x.shape
    return pl.pallas_call(
        pack_kernel,
        grid=(rows // TILE,),
        in_specs=[pl.BlockSpec(post.shape, lambda i: (0, 0)), pl.BlockSpec((tokens, depth), lambda i: (0, 0))],
        out_specs=pl.BlockSpec((TILE, depth // LANES, LANES), lambda i: (i, 0, 0)),
        out_shape=jax.ShapeDtypeStruct((rows, depth // LANES, LANES), BF16),
        cost_estimate=pl.CostEstimate(flops=2 * rows * tokens * depth, bytes_accessed=2 * rows * depth, transcendentals=0),
        name="pack",
    )(post, x)


def expert_kernel(z_ref, gate_ref, up_ref, down_ref, out_ref, rows, flat, acc, in_sem, out_sem):
    f, steps = pl.program_id(0), pl.num_programs(0)
    tiles, depth = rows.shape[0] // TILE, flat.shape[1]

    def fetch(i, r):
        return pltpu.make_async_copy(z_ref.at[r], rows.at[r], in_sem.at[i])

    def put(i, r):
        return pltpu.make_async_copy(rows.at[r], out_ref.at[r], out_sem.at[i])

    @pl.when(f == 0)
    def _():
        for i in range(tiles):
            fetch(i, pl.ds(i * TILE, TILE)).start()

    def body(i, carry):
        r = pl.ds(pl.multiple_of(i * TILE, TILE), TILE)

        @pl.when(f == 0)
        def _():
            fetch(i, r).wait()
            flat[r, :] = rows[r].reshape(TILE, depth)

        z = flat[r, :]
        h = (jax.nn.silu(dot(z, gate_ref[0])) * dot(z, up_ref[0])).astype(BF16)
        part = dot(h, down_ref[0])

        @pl.when(f == 0)
        def _():
            acc[r, :] = part

        @pl.when((f > 0) & (f < steps - 1))
        def _():
            acc[r, :] += part

        @pl.when(f == steps - 1)
        def _():
            rows[r] = (acc[r, :] + part).reshape(TILE, depth // LANES, LANES).astype(BF16)
            put(i, r).start()

        return carry

    lax.fori_loop(0, tiles, body, 0)

    @pl.when(f == steps - 1)
    def _():
        for i in range(tiles):
            put(i, pl.ds(i * TILE, TILE)).wait()


def run_expert(k, z, w_gate, w_up, w_down, width=768):
    rows, depth, inner = z.shape[0], w_gate.shape[1], w_gate.shape[2]
    return pl.pallas_call(
        expert_kernel,
        grid=(inner // width,),
        in_specs=[
            pl.BlockSpec(memory_space=pl.ANY),
            pl.BlockSpec((1, depth, width), lambda f: (k, 0, f)),
            pl.BlockSpec((1, depth, width), lambda f: (k, 0, f)),
            pl.BlockSpec((1, width, depth), lambda f: (k, f, 0)),
        ],
        out_specs=pl.BlockSpec(memory_space=pl.ANY),
        out_shape=jax.ShapeDtypeStruct(z.shape, BF16),
        scratch_shapes=[
            pltpu.VMEM(z.shape, BF16),
            pltpu.VMEM((rows, depth), BF16),
            pltpu.VMEM((rows, depth), F32),
            pltpu.SemaphoreType.DMA((rows // TILE,)),
            pltpu.SemaphoreType.DMA((rows // TILE,)),
        ],
        compiler_params=pltpu.CompilerParams(vmem_limit_bytes=VMEM_LIMIT),
        cost_estimate=pl.CostEstimate(flops=6 * rows * depth * inner, bytes_accessed=6 * depth * inner, transcendentals=0),
        name="expert",
    )(z, w_gate, w_up, w_down)


def combine_kernel(place_ref, gate_ref, rows_ref, *rest):
    before_ref, (y_ref, acc) = (rest[0], rest[1:]) if len(rest) == 3 else (None, rest)
    tokens, depth = y_ref.shape
    i = pl.program_id(0)

    @pl.when(i == 0)
    def _():
        acc[...] = jnp.zeros_like(acc) if before_ref is None else before_ref[...]

    at = iota((tokens, TILE), 1) + i * TILE
    weight = jnp.zeros((tokens, TILE), F32)
    for j in range(place_ref.shape[1]):
        gate = gate_ref[:, j : j + 1].astype(BF16).astype(F32)
        weight = jnp.where(at == place_ref[:, j : j + 1], gate, weight)
    acc[...] += dot(weight.astype(BF16), rows_ref[...].reshape(TILE, depth))

    @pl.when(i == pl.num_programs(0) - 1)
    def _():
        y_ref[...] = acc[...].astype(y_ref.dtype)


def combine(place, gate, rows, before, dtype):
    tokens, depth = gate.shape[0], rows.shape[1] * rows.shape[2]
    whole = lambda a: pl.BlockSpec(a.shape, lambda i: (0, 0))
    extra = [] if before is None else [before]
    return pl.pallas_call(
        combine_kernel,
        grid=(rows.shape[0] // TILE,),
        in_specs=[whole(place), whole(gate), pl.BlockSpec((TILE, *rows.shape[1:]), lambda i: (i, 0, 0))]
        + [whole(a) for a in extra],
        out_specs=pl.BlockSpec((tokens, depth), lambda i: (0, 0)),
        scratch_shapes=[pltpu.VMEM((tokens, depth), F32)],
        out_shape=jax.ShapeDtypeStruct((tokens, depth), dtype),
        cost_estimate=pl.CostEstimate(
            flops=2 * rows.shape[0] * tokens * depth, bytes_accessed=2 * rows.shape[0] * depth, transcendentals=0
        ),
        name="combine",
    )(place, gate, rows, *extra)


def solution(mesh):
    members = mesh.shape["ep"]

    def exchange(rows):
        return lax.all_to_all(rows.reshape(members, -1, *rows.shape[1:]), "ep", 0, 0).reshape(rows.shape)

    def step(x, expert, slot, gate, w_gate, w_up, w_down):
        tokens, depth = x.shape[2:]
        slots = 5 * tokens * expert.shape[3] // (4 * 2 * members)
        x, expert, slot, gate = x[0, 0], expert[0, 0], slot[0, 0], gate[0, 0]
        row = jnp.where(slot < slots, expert // 2 * slots + slot, -1)
        place = [jnp.where(expert % 2 == k, row, -1) for k in (0, 1)]

        out = []
        for k in (0, 1):
            z = exchange(pack(place[k].T, x, members * slots))
            out.append(exchange(run_expert(k, z, w_gate, w_up, w_down)))
        first = combine(place[0], gate, out[0], None, F32)
        return combine(place[1], gate, out[1], first, BF16)[None, None]

    spread, held = P("dp", "ep"), P("ep")
    return jax.shard_map(
        step,
        mesh=mesh,
        in_specs=(spread, spread, spread, spread, held, held, held),
        out_specs=spread,
        check_vma=False,
    )
```

time: 567 us -> 352 us (0.62)
  the two profiles are of different devices: /device:TPU:83 before, /device:TPU:16 now
where the time goes in v1:
time: 352 us
  waiting for transfers between devices  202 us (57%)
  Pallas kernels  107 us (30%)
  starting transfers between devices  38.5 us (11%)
  local copies, waits for them, and re-layouts  3.77 us (1%)
    all_to_all x4, waiting for transfers between devices, exchange(): lax.all_to_all(rows.reshape(members, -1, *rows.shape[1:]), 'ep', 0, 0)  202 us
    pallas_call x2, Pallas kernels, run_expert(): pl.pallas_call(expert_kernel, grid=(inner // width,), in_specs=[pl.BlockS...  77.6 us
    all_to_all x4, starting transfers between devices, exchange(): lax.all_to_all(rows.reshape(members, -1, *rows.shape[1:]), 'ep', 0, 0)  38.5 us
    pallas_call x2, Pallas kernels, combine(): pl.pallas_call(combine_kernel, grid=(rows.shape[0] // TILE,), in_specs=[w...  16.6 us
    pallas_call x2, Pallas kernels, pack(): pl.pallas_call(pack_kernel, grid=(rows // TILE,), in_specs=[pl.BlockSpec(...  13.3 us
  transfers between devices with their start and end apart: 4, of which 4 were waited for; matrix products, arithmetic and copies ran while one was open for 0% of the time, Pallas kernels for 26%

profile of v1, /device:TPU:16, one launch (start us, length us, event | category | flops | bytes accessed | tf_op | source)
XLA Modules:
  0.0 351.6 jit_solution(18081150432507066902)
XLA Ops:
  0.0 0.8 copy.8
  0.8 0.8 copy.9
  1.7 0.1 compare_select_fusion
  1.8 0.0 copy-start.1
  1.8 0.0 copy-start
  1.8 0.7 copy.12.post_ref
  2.5 6.7 %pack.3 = bf16[1280,16,128]{2,1,0:T(8,128)(2,1)} custom-call(s32[8,256]{1,0:T(8,128)} %copy.12.post_ref, bf16[256,2048]{1,0:T(8,128)(2,1)} %bitcast.60), custom_call_target="tpu_custom_call" | custom-call | flops 1342177280 | bytes 5242880 | tf_op jit(solution)/shard_map/pack/pallas_call | solution.py:36
  9.2 0.0 copy-done.1
  9.2 11.5 %all-to-all-start.2 = ((bf16[64,20,16,128]{3,2,1,0:T(8,128)(2,1)}), bf16[64,20,16,128]{3,2,1,0:T(8,128)(2,1)}, u32[]{:S(2)}, u32[]{:S(2)}) async-start(bf16[64,20,16,128]{3,2,1,0:T(8,128)(2,1)} %bitcast.57), calls=%async_computation.2 | async-start | bytes 10485760 | tf_op jit(solution)/shard_map/all_to_all | solution.py:167
  20.6 0.0 copy-done
  20.7 0.7 copy.11.post_ref
  21.3 6.6 %pack.2 = bf16[1280,16,128]{2,1,0:T(8,128)(2,1)} custom-call(s32[8,256]{1,0:T(8,128)} %copy.11.post_ref, bf16[256,2048]{1,0:T(8,128)(2,1)} %bitcast.61), custom_call_target="tpu_custom_call" | custom-call | flops 1342177280 | bytes 5242880 | tf_op jit(solution)/shard_map/pack/pallas_call | solution.py:36
  27.9 66.7 %all-to-all-done.2 = bf16[64,20,16,128]{3,2,1,0:T(8,128)(2,1)} async-done(((bf16[64,20,16,128]{3,2,1,0:T(8,128)(2,1)}), bf16[64,20,16,128]{3,2,1,0:T(8,128)(2,1)}, u32[]{:S(2)}, u32[]{:S(2)}) %all-to-all-start.2) | async-done | bytes 5242912 | tf_op jit(solution)/shard_map/all_to_all | solution.py:167
  94.6 10.3 %all-to-all-start = ((bf16[64,20,16,128]{3,2,1,0:T(8,128)(2,1)}), bf16[64,20,16,128]{3,2,1,0:T(8,128)(2,1)}, u32[]{:S(2)}, u32[]{:S(2)}) async-start(bf16[64,20,16,128]{3,2,1,0:T(8,128)(2,1)} %bitcast.56), calls=%async_computation | async-start | bytes 10485760 | tf_op jit(solution)/shard_map/all_to_all | solution.py:167
  104.9 38.8 %expert.3 = bf16[1280,16,128]{2,1,0:T(8,128)(2,1)} custom-call(bf16[1280,16,128]{2,1,0:T(8,128)(2,1)} %bitcast.11.z_ref, bf16[2,2048,1536]{2,1,0:T(8,128)(2,1)} %gate_ref.3, bf16[2,2048,1536]{2,1,0:T(8,128)(2,1)} %up_ref.3, bf16[2,1536,2048]{2,1,0:T(8,128)(2,1)} %down_ref.3), custom_call_target="tpu_custom_call" | custom-call | flops 24159191040 | bytes 18874368 | tf_op jit(solution)/shard_map/expert/pallas_call | solution.py:99
  143.7 28.6 %all-to-all-done = bf16[64,20,16,128]{3,2,1,0:T(8,128)(2,1)} async-done(((bf16[64,20,16,128]{3,2,1,0:T(8,128)(2,1)}), bf16[64,20,16,128]{3,2,1,0:T(8,128)(2,1)}, u32[]{:S(2)}, u32[]{:S(2)}) %all-to-all-start) | async-done | bytes 5242912 | tf_op jit(solution)/shard_map/all_to_all | solution.py:167
  172.3 9.7 %all-to-all-start.3 = ((bf16[64,20,16,128]{3,2,1,0:T(8,128)(2,1)}), bf16[64,20,16,128]{3,2,1,0:T(8,128)(2,1)}, u32[]{:S(2)}, u32[]{:S(2)}) async-start(bf16[64,20,16,128]{3,2,1,0:T(8,128)(2,1)} %bitcast.59), calls=%async_computation.3 | async-start | bytes 10485760 | tf_op jit(solution)/shard_map/all_to_all | solution.py:167
  182.0 38.8 %expert.2 = bf16[1280,16,128]{2,1,0:T(8,128)(2,1)} custom-call(bf16[1280,16,128]{2,1,0:T(8,128)(2,1)} %bitcast.6.z_ref, bf16[2,2048,1536]{2,1,0:T(8,128)(2,1)} %gate_ref.3, bf16[2,2048,1536]{2,1,0:T(8,128)(2,1)} %up_ref.3, bf16[2,1536,2048]{2,1,0:T(8,128)(2,1)} %down_ref.3), custom_call_target="tpu_custom_call" | custom-call | flops 24159191040 | bytes 18874368 | tf_op jit(solution)/shard_map/expert/pallas_call | solution.py:99
  220.8 36.8 %all-to-all-done.3 = bf16[64,20,16,128]{3,2,1,0:T(8,128)(2,1)} async-done(((bf16[64,20,16,128]{3,2,1,0:T(8,128)(2,1)}), bf16[64,20,16,128]{3,2,1,0:T(8,128)(2,1)}, u32[]{:S(2)}, u32[]{:S(2)}) %all-to-all-start.3) | async-done | bytes 5242912 | tf_op jit(solution)/shard_map/all_to_all | solution.py:167
  257.6 0.0 copy-start.2
  257.6 7.1 %all-to-all-start.1 = ((bf16[64,20,16,128]{3,2,1,0:T(8,128)(2,1)}), bf16[64,20,16,128]{3,2,1,0:T(8,128)(2,1)}, u32[]{:S(2)}, u32[]{:S(2)}) async-start(bf16[64,20,16,128]{3,2,1,0:T(8,128)(2,1)} %bitcast.58), calls=%async_computation.1 | async-start | bytes 10485760 | tf_op jit(solution)/shard_map/all_to_all | solution.py:167
  264.7 0.0 copy-done.2
  264.7 0.8 copy.10
  265.5 8.1 %combine.2.rest_0_ = f32[256,2048]{1,0:T(8,128)} custom-call(s32[256,8]{1,0:T(8,128)} %copy-done.1, f32[256,8]{1,0:T(8,128)} %bitcast.63, bf16[1280,16,128]{2,1,0:T(8,128)(2,1)} %bitcast.13.rows_ref), custom_call_target="tpu_custom_call" | custom-call | flops 1342177280 | bytes 5242880 | tf_op jit(solution)/shard_map/combine/pallas_call | solution.py:148
  273.6 69.6 %all-to-all-done.1 = bf16[64,20,16,128]{3,2,1,0:T(8,128)(2,1)} async-done(((bf16[64,20,16,128]{3,2,1,0:T(8,128)(2,1)}), bf16[64,20,16,128]{3,2,1,0:T(8,128)(2,1)}, u32[]{:S(2)}, u32[]{:S(2)}) %all-to-all-start.1) | async-done | bytes 5242912 | tf_op jit(solution)/shard_map/all_to_all | solution.py:167
  343.1 8.5 %combine.3 = bf16[256,2048]{1,0:T(8,128)(2,1)} custom-call(s32[256,8]{1,0:T(8,128)} %copy-done, f32[256,8]{1,0:T(8,128)} %bitcast.64, bf16[1280,16,128]{2,1,0:T(8,128)(2,1)} %bitcast.8.rows_ref, f32[256,2048]{1,0:T(8,128)} %combine.2.rest_0_), custom_call_target="tpu_custom_call" | custom-call | flops 1342177280 | bytes 5242880 | tf_op jit(solution)/shard_map/combine/pallas_call | solution.py:148
Async XLA Ops:
  1.8 7.4 %copy-start.1 = (s32[256,8]{1,0:T(8,128)}, s32[256,8]{1,0:T(8,128)S(1)}, u32[]{:S(2)}) copy-start(s32[256,8]{1,0:T(8,128)S(1)} %get-tuple-element.5.place_ref) | copy-start | bytes 24580
  1.8 18.8 %copy-start = (s32[256,8]{1,0:T(8,128)}, s32[256,8]{1,0:T(8,128)S(1)}, u32[]{:S(2)}) copy-start(s32[256,8]{1,0:T(8,128)S(1)} %get-tuple-element.6.place_ref) | copy-start | bytes 24580
  9.2 85.5 %all-to-all-start.2 = ((bf16[64,20,16,128]{3,2,1,0:T(8,128)(2,1)}), bf16[64,20,16,128]{3,2,1,0:T(8,128)(2,1)}, u32[]{:S(2)}, u32[]{:S(2)}) async-start(bf16[64,20,16,128]{3,2,1,0:T(8,128)(2,1)} %bitcast.57), calls=%async_computation.2 | async-start | bytes 10485760 | tf_op jit(solution)/shard_map/all_to_all | solution.py:167
  94.6 77.7 %all-to-all-start = ((bf16[64,20,16,128]{3,2,1,0:T(8,128)(2,1)}), bf16[64,20,16,128]{3,2,1,0:T(8,128)(2,1)}, u32[]{:S(2)}, u32[]{:S(2)}) async-start(bf16[64,20,16,128]{3,2,1,0:T(8,128)(2,1)} %bitcast.56), calls=%async_computation | async-start | bytes 10485760 | tf_op jit(solution)/shard_map/all_to_all | solution.py:167
  172.3 85.3 %all-to-all-start.3 = ((bf16[64,20,16,128]{3,2,1,0:T(8,128)(2,1)}), bf16[64,20,16,128]{3,2,1,0:T(8,128)(2,1)}, u32[]{:S(2)}, u32[]{:S(2)}) async-start(bf16[64,20,16,128]{3,2,1,0:T(8,128)(2,1)} %bitcast.59), calls=%async_computation.3 | async-start | bytes 10485760 | tf_op jit(solution)/shard_map/all_to_all | solution.py:167
  257.6 7.1 %copy-start.2 = (f32[1,1,256,8]{2,3,1,0:T(8,128)S(1)}, f32[1,1,256,8]{2,3,1,0:T(8,128)}, u32[]{:S(2)}) copy-start(f32[1,1,256,8]{2,3,1,0:T(8,128)} %param.10) | copy-start | bytes 24580
  257.6 85.5 %all-to-all-start.1 = ((bf16[64,20,16,128]{3,2,1,0:T(8,128)(2,1)}), bf16[64,20,16,128]{3,2,1,0:T(8,128)(2,1)}, u32[]{:S(2)}, u32[]{:S(2)}) async-start(bf16[64,20,16,128]{3,2,1,0:T(8,128)(2,1)} %bitcast.58), calls=%async_computation.1 | async-start | bytes 10485760 | tf_op jit(solution)/shard_map/all_to_all | solution.py:167

commit v2 on v0

v2 whole, which is shorter than its diff:
```python
import functools

import jax
import jax.numpy as jnp
from jax import lax
from jax.experimental import pallas as pl
from jax.experimental.pallas import tpu as pltpu
from jax.sharding import PartitionSpec as P

F32, BF16, I32 = jnp.float32, jnp.bfloat16, jnp.int32
MESH = pl.DeviceIdType.MESH
SIDE = 4
STRIDE = (SIDE * SIDE, SIDE, 1)
AXES = ((0, 1, 2), (1, 2, 0), (2, 0, 1))
GROUP = 4
WIDTH = 512
PARTS, OTHERS = range(3), range(1, SIDE)


def iota(shape, dim):
    return lax.broadcasted_iota(I32, shape, dim)


def dot(a, b):
    return jnp.dot(a, b, preferred_element_type=F32)


def kernel(slots, cols, width, meta_ref, x_ref, gate_hbm, up_hbm, down_hbm, y_ref, *rest):
    relay, back, home = rest[0:3], rest[3:6], rest[6:9]
    spread, boxes, rows, sums = rest[9:12], rest[12:15], rest[15:18], rest[18:21]
    metas, flat, acc, gate_w, up_w, down_w = rest[21:27]
    (bell_s, bell_r, tok_s, tok_r, two_s, two_r, three_s, three_r) = rest[27:35]
    (b3_s, b3_r, b2_s, b2_r, end_s, end_r, own, w_sem) = rest[35:43]

    tokens, depth = x_ref.shape
    top = meta_ref.shape[0] // 2
    inner = gate_hbm.shape[2]
    steps = inner // width
    plane = SIDE * SIDE * slots
    offset = [sum(cols[:c]) for c in PARTS]
    me, dp = lax.axis_index("ep"), lax.axis_index("dp")
    at = (me // STRIDE[0], lax.rem(me // STRIDE[1], SIDE), lax.rem(me, SIDE))

    def other(axis, d):
        return lax.rem(at[axis] + d, SIDE)

    def remote(src, dst, send, recv, axis, d):
        target = me + (other(axis, d) - at[axis]) * STRIDE[axis]
        return pltpu.make_async_remote_copy(
            src_ref=src, dst_ref=dst, send_sem=send, recv_sem=recv, device_id=(dp, target), device_id_type=MESH
        )


    def third(ref, c, p):
        return (ref.at[:, :, p], ref.at[p], ref.at[:, p])[c]

    def second(ref, c, p):
        return ref.at[p] if c == 2 else ref.at[:, p]


    def bell(c, d):
        return remote(meta_ref, metas.at[c, at[AXES[c][0]]], bell_s.at[c, d - 1], bell_r.at[c, d - 1], AXES[c][0], d)

    def token(c, d):
        src = x_ref.at[:, pl.ds(offset[c], cols[c])]
        return remote(src, spread[c].at[at[AXES[c][0]]], tok_s.at[c, d - 1], tok_r.at[c, d - 1], AXES[c][0], d)

    def two(k, c, d):
        axis = AXES[c][1]
        src, dst = boxes[c].at[other(axis, d)], second(relay[c].at[k], c, at[axis])
        return remote(src, dst, two_s.at[k, c, d - 1], two_r.at[k, c, d - 1], axis, d)

    def two_own(k, c):
        p = at[AXES[c][1]]
        return pltpu.make_async_copy(boxes[c].at[p], second(relay[c].at[k], c, p), own.at[0, k, c])

    def three(k, c, d):
        axis = AXES[c][2]
        src, dst = relay[c].at[k, :, :, other(axis, d)], third(rows[c].at[k], c, at[axis])
        return remote(src, dst, three_s.at[k, c, d - 1], three_r.at[k, c, d - 1], axis, d)

    def three_own(k, c):
        p = at[AXES[c][2]]
        return pltpu.make_async_copy(relay[c].at[k, :, :, p], third(rows[c].at[k], c, p), own.at[1, k, c])

    def back_three(k, c, d):
        axis = AXES[c][2]
        src, dst = third(rows[c].at[k], c, other(axis, d)), back[c].at[k, at[axis]]
        return remote(src, dst, b3_s.at[k, c, d - 1], b3_r.at[k, c, d - 1], axis, d)

    def back_three_own(k, c):
        p = at[AXES[c][2]]
        return pltpu.make_async_copy(third(rows[c].at[k], c, p), back[c].at[k, p], own.at[2, k, c])

    def returned(k, c, p):
        return back[c].at[k, :, p] if c == 2 else back[c].at[k, :, :, p]

    def back_two(k, c, d):
        axis = AXES[c][1]
        src, dst = returned(k, c, other(axis, d)), home[c].at[k, at[axis]]
        return remote(src, dst, b2_s.at[k, c, d - 1], b2_r.at[k, c, d - 1], axis, d)

    def load_home(k, c, d):
        p = other(AXES[c][1], SIDE - d)
        src = returned(k, c, p) if d == 0 else home[c].at[k, p]
        return pltpu.make_async_copy(src, boxes[c].at[p], own.at[3 + d, k, c])

    def end(c, d):
        axis = AXES[c][0]
        src, dst = spread[c].at[other(axis, d)], sums[c].at[at[axis]]
        return remote(src, dst, end_s.at[c, d - 1], end_r.at[c, d - 1], axis, d)

    def weights(n):
        k, cut, s = n // steps, pl.ds(lax.rem(n, steps) * width, width), lax.rem(n, 2)
        return (
            pltpu.make_async_copy(gate_hbm.at[k, :, cut], gate_w.at[s], w_sem.at[s, 0]),
            pltpu.make_async_copy(up_hbm.at[k, :, cut], up_w.at[s], w_sem.at[s, 1]),
            pltpu.make_async_copy(down_hbm.at[k, cut, :], down_w.at[s], w_sem.at[s, 2]),
        )


    def place_of_row(k, c):
        r = iota((plane, tokens), 0)
        a1, a2, a3 = AXES[c]
        device = at[a1] * STRIDE[a1] + r // (SIDE * slots) * STRIDE[a2] + r // slots % SIDE * STRIDE[a3]
        return ((2 * device + k) * slots + r % slots).astype(F32)

    def pack(k, c):
        place = place_of_row(k, c)

        def one(s, carry):
            hit = place == metas[c, s, 0:1, :]
            for j in range(1, top):
                hit = hit | (place == metas[c, s, j : j + 1, :])
            out = dot(jnp.where(hit, 1.0, 0.0).astype(BF16), spread[c][s]).astype(BF16)
            boxes[c][:, s] = out.reshape(SIDE, SIDE, slots // GROUP, GROUP, cols[c])
            return carry

        lax.fori_loop(0, SIDE, one, 0)

    def combine(k, c):
        place = place_of_row(k, c)
        span = pl.ds(offset[c], cols[c])

        def one(s, carry):
            weight = jnp.zeros((plane, tokens), F32)
            for j in range(top):
                gate = metas[c, s, top + j : top + j + 1, :].astype(BF16).astype(F32)
                weight = jnp.where(place == metas[c, s, j : j + 1, :], gate, weight)
            got = boxes[c][:, :, s].reshape(plane, cols[c])
            part = lax.dot_general(
                weight.astype(BF16), got, (((0,), (0,)), ((), ())), preferred_element_type=F32
            )
            r = pl.ds(pl.multiple_of(s * tokens, tokens), tokens)
            if k == 0:
                acc[r, span] = part
            else:
                acc[r, span] += part
                spread[c][s] = acc[r, span].astype(BF16)
            return carry

        lax.fori_loop(0, SIDE, one, 0)

    def expert(k, between):
        tile = plane

        def step(f):
            n = k * steps + f
            s = lax.rem(n, 2)
            if n + 1 < 2 * steps:
                for copy in weights(n + 1):
                    copy.start()
            for copy in weights(n):
                copy.wait()

            def body(i, carry):
                r = pl.ds(pl.multiple_of(i * tile, tile), tile)
                if f == 0:
                    for c in PARTS:
                        flat[r, pl.ds(offset[c], cols[c])] = rows[c][k, i].reshape(tile, cols[c])
                z = flat[r, :]
                h = (jax.nn.silu(dot(z, gate_w[s])) * dot(z, up_w[s])).astype(BF16)
                part = dot(h, down_w[s])
                if f == 0:
                    acc[r, :] = part
                elif f < steps - 1:
                    acc[r, :] += part
                else:
                    flat[r, :] = (acc[r, :] + part).astype(BF16)
                    for c in PARTS:
                        out = flat[r, pl.ds(offset[c], cols[c])]
                        rows[c][k, i] = out.reshape(SIDE, SIDE, slots // GROUP, GROUP, cols[c])
                return carry

            lax.fori_loop(0, SIDE, body, 0)

        for f in range(steps):
            step(f)
            between(f)


    barrier = pltpu.get_barrier_semaphore()
    for axis in range(3):
        for d in OTHERS:
            target = me + (other(axis, d) - at[axis]) * STRIDE[axis]
            pl.semaphore_signal(barrier, inc=1, device_id=(dp, target), device_id_type=MESH)
    for copy in weights(0):
        copy.start()
    for c in PARTS:
        metas[c, at[AXES[c][0]]] = meta_ref[...]
        spread[c][at[AXES[c][0]]] = x_ref[:, pl.ds(offset[c], cols[c])]
    pl.semaphore_wait(barrier, 3 * (SIDE - 1))

    for c in PARTS:
        for d in OTHERS:
            bell(c, d).start()
            token(c, d).start()

    def relay_two(k, c):
        two_own(k, c).wait()
        for d in OTHERS:
            two(k, c, d).wait()
        for d in OTHERS:
            three(k, c, d).start()
        three_own(k, c).start()

    def send_boxes(k, c):
        pack(k, c)
        for d in OTHERS:
            two(k, c, d).start()
        two_own(k, c).start()

    for c in PARTS:
        for d in OTHERS:
            bell(c, d).wait()
            token(c, d).wait()
        send_boxes(0, c)
    for c in PARTS:
        relay_two(0, c)
        send_boxes(1, c)

    def wait_rows(k):
        for c in PARTS:
            for d in OTHERS:
                three(k, c, d).wait()
            three_own(k, c).wait()

    def send_back(k):
        for c in PARTS:
            for d in OTHERS:
                back_three(k, c, d).start()
            back_three_own(k, c).start()

    def relay_back(k, c):
        back_three_own(k, c).wait()
        for d in OTHERS:
            back_three(k, c, d).wait()
        for d in OTHERS:
            back_two(k, c, d).start()

    def bring_home(k, c):
        load_home(k, c, 0).start()
        for d in OTHERS:
            back_two(k, c, d).wait()
            load_home(k, c, d).start()
        for d in range(SIDE):
            load_home(k, c, d).wait()
        combine(k, c)

    def during_first(f):
        if f == 0:
            for c in PARTS:
                relay_two(1, c)

    def during_second(f):
        if f == steps - 2:
            for c in PARTS:
                relay_back(0, c)

    wait_rows(0)
    expert(0, during_first)
    send_back(0)
    wait_rows(1)
    expert(1, during_second)
    send_back(1)
    for c in PARTS:
        bring_home(0, c)
    for c in PARTS:
        relay_back(1, c)
    for c in PARTS:
        bring_home(1, c)
        for d in OTHERS:
            end(c, d).start()
    for c in PARTS:
        span = pl.ds(offset[c], cols[c])
        axis = AXES[c][0]
        total = acc[pl.ds(pl.multiple_of(at[axis] * tokens, tokens), tokens), span]
        for d in OTHERS:
            end(c, d).wait()
        for d in OTHERS:
            total += sums[c][other(axis, d)].astype(F32)
        y_ref[:, span] = total.astype(y_ref.dtype)


def moe(meta, x, w_gate, w_up, w_down, slots):
    (tokens, depth), inner = x.shape, w_gate.shape[2]
    third = depth // 128 // 3 * 128
    cols = (third, third, depth - 2 * third)
    width = min(WIDTH, inner // 2)
    plane = SIDE * SIDE * slots
    box = lambda c, *lead: (*lead, SIDE, SIDE, SIDE, slots // GROUP, GROUP, cols[c])
    hbm = [jax.ShapeDtypeStruct(box(c, 2), BF16) for _ in range(3) for c in PARTS]
    dma = pltpu.SemaphoreType.DMA
    n = SIDE - 1
    out = pl.pallas_call(
        functools.partial(kernel, slots, cols, width),
        in_specs=[pl.BlockSpec(memory_space=pltpu.VMEM)] * 2 + [pl.BlockSpec(memory_space=pl.ANY)] * 3,
        out_specs=[pl.BlockSpec(memory_space=pltpu.VMEM)] + [pl.BlockSpec(memory_space=pl.ANY)] * len(hbm),
        out_shape=[jax.ShapeDtypeStruct((tokens, depth), BF16)] + hbm,
        scratch_shapes=[pltpu.VMEM((SIDE, tokens, cols[c]), BF16) for c in PARTS]
        + [pltpu.VMEM(box(c), BF16) for c in PARTS]
        + [pltpu.VMEM(box(c, 2), BF16) for c in PARTS]
        + [pltpu.VMEM((SIDE, tokens, cols[c]), BF16) for c in PARTS]
        + [
            pltpu.VMEM((3, SIDE, *meta.shape), F32),
            pltpu.VMEM((SIDE * plane, depth), BF16),
            pltpu.VMEM((SIDE * plane, depth), F32),
            pltpu.VMEM((2, depth, width), BF16),
            pltpu.VMEM((2, depth, width), BF16),
            pltpu.VMEM((2, width, depth), BF16),
        ]
        + [dma((3, n))] * 4
        + [dma((2, 3, n))] * 8
        + [dma((3, n))] * 2
        + [dma((3 + SIDE, 2, 3)), dma((2, 3))],
        compiler_params=pltpu.CompilerParams(
            collective_id=0, has_side_effects=True, vmem_limit_bytes=67043328
        ),
        name="moe",
    )(meta, x, w_gate, w_up, w_down)
    return out[0]


def solution(mesh):
    members = mesh.shape["ep"]

    def step(x, expert, slot, gate, w_gate, w_up, w_down):
        tokens = x.shape[2]
        slots = 5 * tokens * expert.shape[3] // (4 * 2 * members)
        x, expert, slot, gate = x[0, 0], expert[0, 0], slot[0, 0], gate[0, 0]
        place = jnp.where(slot < slots, expert * slots + slot, -1)
        meta = jnp.concatenate([place.astype(F32).T, gate.T])
        return moe(meta, x, w_gate, w_up, w_down, slots)[None, None]

    spread, held = P("dp", "ep"), P("ep")
    return jax.shard_map(
        step,
        mesh=mesh,
        in_specs=(spread, spread, spread, spread, held, held, held),
        out_specs=spread,
        check_vma=False,
    )
```

time: 567 us -> 241 us (0.43)
  the two profiles are of different devices: /device:TPU:83 before, /device:TPU:0 now
where the time goes in v2:
time: 241 us
  Pallas kernels  236 us (98%)
    pallas_call x1, Pallas kernels, moe(): pl.pallas_call(functools.partial(kernel, slots, cols, width), in_specs=[p...  236 us

profile of v2, /device:TPU:0, one launch (start us, length us, event | category | flops | bytes accessed | tf_op | source)
XLA Modules:
  0.0 240.8 jit_solution(8912781740184125455)
XLA Ops:
  0.0 0.7 convert_bitcast_fusion
  0.7 1.3 pad_maximum_fusion.meta_ref
  2.0 236.5 %moe.1 = (bf16[256,2048]{1,0:T(8,128)(2,1)}, bf16[2,4,4,4,5,4,640]{6,5,4,3,2,1,0:T(4,128)(2,1)}, bf16[2,4,4,4,5,4,640]{6,5,4,3,2,1,0:T(4,128)(2,1)}, bf16[2,4,4,...) custom-call(f32[16,256]{1,0:T(8,128)} %pad_maximum_fusion.meta_ref, ...), custom_call_target="tpu_custom_call" | custom-call | tf_op jit(solution)/shard_map/moe/pallas_call | solution.py:315
  238.5 2.3 copy.9

commit v3 on v2

--- a/solution.py
+++ b/solution.py
@@ -1,3 +1,4 @@
+import contextlib
 import functools
 
 import jax
@@ -11,10 +12,15 @@
 MESH = pl.DeviceIdType.MESH
 SIDE = 4
 STRIDE = (SIDE * SIDE, SIDE, 1)
-AXES = ((0, 1, 2), (1, 2, 0), (2, 0, 1))
+AXES = ((0, 1, 2), (1, 2, 0), (2, 0, 1)) * 2
 GROUP = 4
 WIDTH = 512
-PARTS, OTHERS = range(3), range(1, SIDE)
+PARTS, ORDERS, OTHERS = range(6), range(3), range(1, SIDE)
+FIRST, SECOND = (4, 4, 5, 5, 6, 7), (2, 3, 4, 5, 6, 7)
+
+
+def phase(name):
+    return contextlib.nullcontext()
 
 
 def iota(shape, dim):
@@ -26,11 +32,12 @@
 
 
 def kernel(slots, cols, width, meta_ref, x_ref, gate_hbm, up_hbm, down_hbm, y_ref, *rest):
-    relay, back, home = rest[0:3], rest[3:6], rest[6:9]
-    spread, boxes, rows, sums = rest[9:12], rest[12:15], rest[15:18], rest[18:21]
-    metas, flat, acc, gate_w, up_w, down_w = rest[21:27]
-    (bell_s, bell_r, tok_s, tok_r, two_s, two_r, three_s, three_r) = rest[27:35]
-    (b3_s, b3_r, b2_s, b2_r, end_s, end_r, own, w_sem) = rest[35:43]
+    rest = list(rest)
+    take = lambda n: [rest.pop(0) for _ in range(n)]
+    relay, back, home, spread, boxes, rows, sums = (take(len(PARTS)) for _ in range(7))
+    metas, mask, flat, acc, gate_w, up_w, down_w = take(7)
+    bell_s, bell_r, tok_s, tok_r, two_s, two_r, three_s, three_r = take(8)
+    b3_s, b3_r, b2_s, b2_r, end_s, end_r, own, w_sem = take(8)
 
     tokens, depth = x_ref.shape
     top = meta_ref.shape[0] // 2
@@ -39,23 +46,26 @@
     plane = SIDE * SIDE * slots
     offset = [sum(cols[:c]) for c in PARTS]
     me, dp = lax.axis_index("ep"), lax.axis_index("dp")
-    at = (me // STRIDE[0], lax.rem(me // STRIDE[1], SIDE), lax.rem(me, SIDE))
+    turn = lax.rem(dp, 2)
+    chip = (me // STRIDE[0], lax.rem(me // STRIDE[1], SIDE), lax.rem(me, SIDE))
+    turned = lambda v: tuple(v[i] + turn * (v[(i + 1) % 3] - v[i]) for i in range(3))
+    at, stride = turned(chip), turned(STRIDE)
 
     def other(axis, d):
         return lax.rem(at[axis] + d, SIDE)
 
     def remote(src, dst, send, recv, axis, d):
-        target = me + (other(axis, d) - at[axis]) * STRIDE[axis]
+        target = me + (other(axis, d) - at[axis]) * stride[axis]
         return pltpu.make_async_remote_copy(
             src_ref=src, dst_ref=dst, send_sem=send, recv_sem=recv, device_id=(dp, target), device_id_type=MESH
         )
 
 
     def third(ref, c, p):
-        return (ref.at[:, :, p], ref.at[p], ref.at[:, p])[c]
+        return (ref.at[:, :, p], ref.at[p], ref.at[:, p])[c % 3]
 
     def second(ref, c, p):
-        return ref.at[p] if c == 2 else ref.at[:, p]
+        return ref.at[p] if c % 3 == 2 else ref.at[:, p]
 
 
     def bell(c, d):
@@ -93,7 +103,7 @@
         return pltpu.make_async_copy(third(rows[c].at[k], c, p), back[c].at[k, p], own.at[2, k, c])
 
     def returned(k, c, p):
-        return back[c].at[k, :, p] if c == 2 else back[c].at[k, :, :, p]
+        return back[c].at[k, :, p] if c % 3 == 2 else back[c].at[k, :, :, p]
 
     def back_two(k, c, d):
         axis = AXES[c][1]
@@ -122,46 +132,60 @@
     def place_of_row(k, c):
         r = iota((plane, tokens), 0)
         a1, a2, a3 = AXES[c]
-        device = at[a1] * STRIDE[a1] + r // (SIDE * slots) * STRIDE[a2] + r // slots % SIDE * STRIDE[a3]
+        device = at[a1] * stride[a1] + r // (SIDE * slots) * stride[a2] + r // slots % SIDE * stride[a3]
         return ((2 * device + k) * slots + r % slots).astype(F32)
 
-    def pack(k, c):
+    def choose(k, c):
         place = place_of_row(k, c)
 
         def one(s, carry):
             hit = place == metas[c, s, 0:1, :]
             for j in range(1, top):
                 hit = hit | (place == metas[c, s, j : j + 1, :])
-            out = dot(jnp.where(hit, 1.0, 0.0).astype(BF16), spread[c][s]).astype(BF16)
-            boxes[c][:, s] = out.reshape(SIDE, SIDE, slots // GROUP, GROUP, cols[c])
+            mask[c, s] = jnp.where(hit, 1.0, 0.0).astype(BF16)
             return carry
 
         lax.fori_loop(0, SIDE, one, 0)
 
-    def combine(k, c):
+    def weigh(k, c):
         place = place_of_row(k, c)
-        span = pl.ds(offset[c], cols[c])
 
         def one(s, carry):
             weight = jnp.zeros((plane, tokens), F32)
             for j in range(top):
                 gate = metas[c, s, top + j : top + j + 1, :].astype(BF16).astype(F32)
                 weight = jnp.where(place == metas[c, s, j : j + 1, :], gate, weight)
+            mask[c, s] = weight.astype(BF16)
+            return carry
+
+        lax.fori_loop(0, SIDE, one, 0)
+
+    def pack(c):
+        def one(s, carry):
+            out = dot(mask[c % 3, s], spread[c][s]).astype(BF16)
+            boxes[c][:, s] = out.reshape(SIDE, SIDE, slots // GROUP, GROUP, cols[c])
+            return carry
+
+        lax.fori_loop(0, SIDE, one, 0)
+
+    def combine(k, c):
+        span = pl.ds(offset[c], cols[c])
+
+        def one(s, carry):
             got = boxes[c][:, :, s].reshape(plane, cols[c])
-            part = lax.dot_general(
-                weight.astype(BF16), got, (((0,), (0,)), ((), ())), preferred_element_type=F32
-            )
+            part = lax.dot_general(mask[c % 3, s], got, (((0,), (0,)), ((), ())), preferred_element_type=F32)
             r = pl.ds(pl.multiple_of(s * tokens, tokens), tokens)
             if k == 0:
                 acc[r, span] = part
             else:
-                acc[r, span] += part
-                spread[c][s] = acc[r, span].astype(BF16)
+                part += acc[r, span]
+                acc[r, span] = part
+                spread[c][s] = part.astype(BF16)
             return carry
 
         lax.fori_loop(0, SIDE, one, 0)
 
-    def expert(k, between):
+    def expert(k, errands):
         tile = plane
 
         def step(f):
@@ -190,30 +214,37 @@
                     for c in PARTS:
                         out = flat[r, pl.ds(offset[c], cols[c])]
                         rows[c][k, i] = out.reshape(SIDE, SIDE, slots // GROUP, GROUP, cols[c])
+                for when, errand in errands:
+                    if when // SIDE == f:
+                        pl.when(i == when % SIDE)(errand)
                 return carry
 
             lax.fori_loop(0, SIDE, body, 0)
 
         for f in range(steps):
-            step(f)
-            between(f)
+            with phase(f"expert_{k}{f}"):
+                step(f)
 
 
     barrier = pltpu.get_barrier_semaphore()
     for axis in range(3):
         for d in OTHERS:
-            target = me + (other(axis, d) - at[axis]) * STRIDE[axis]
+            target = me + (other(axis, d) - at[axis]) * stride[axis]
             pl.semaphore_signal(barrier, inc=1, device_id=(dp, target), device_id_type=MESH)
     for copy in weights(0):
         copy.start()
-    for c in PARTS:
+    for c in ORDERS:
         metas[c, at[AXES[c][0]]] = meta_ref[...]
+    for c in PARTS:
         spread[c][at[AXES[c][0]]] = x_ref[:, pl.ds(offset[c], cols[c])]
-    pl.semaphore_wait(barrier, 3 * (SIDE - 1))
-
-    for c in PARTS:
-        for d in OTHERS:
+    with phase("barrier"):
+        pl.semaphore_wait(barrier, 3 * (SIDE - 1))
+
+    for d in OTHERS:
+        for c in ORDERS:
             bell(c, d).start()
+    for c in PARTS:
+        for d in OTHERS:
             token(c, d).start()
 
     def relay_two(k, c):
@@ -225,19 +256,34 @@
         three_own(k, c).start()
 
     def send_boxes(k, c):
-        pack(k, c)
+        pack(c)
         for d in OTHERS:
             two(k, c, d).start()
         two_own(k, c).start()
 
-    for c in PARTS:
-        for d in OTHERS:
-            bell(c, d).wait()
-            token(c, d).wait()
-        send_boxes(0, c)
-    for c in PARTS:
-        relay_two(0, c)
-        send_boxes(1, c)
+    for c in ORDERS:
+        with phase(f"choose_0{c}"):
+            for d in OTHERS:
+                bell(c, d).wait()
+            choose(0, c)
+    for c in PARTS:
+        with phase(f"spread_wait_{c}"):
+            for d in OTHERS:
+                token(c, d).wait()
+        with phase(f"pack_0{c}"):
+            send_boxes(0, c)
+    with phase("choose_1"):
+        for c in ORDERS:
+            choose(1, c)
+    for c in PARTS:
+        with phase(f"relay_two_0{c}"):
+            relay_two(0, c)
+    for c in PARTS:
+        with phase(f"pack_1{c}"):
+            send_boxes(1, c)
+    with phase("weigh_0"):
+        for c in ORDERS:
+            weigh(0, c)
 
     def wait_rows(k):
         for c in PARTS:
@@ -259,34 +305,50 @@
             back_two(k, c, d).start()
 
     def bring_home(k, c):
-        load_home(k, c, 0).start()
-        for d in OTHERS:
-            back_two(k, c, d).wait()
-            load_home(k, c, d).start()
-        for d in range(SIDE):
-            load_home(k, c, d).wait()
-        combine(k, c)
-
-    def during_first(f):
-        if f == 0:
-            for c in PARTS:
-                relay_two(1, c)
-
-    def during_second(f):
-        if f == steps - 2:
-            for c in PARTS:
-                relay_back(0, c)
-
-    wait_rows(0)
-    expert(0, during_first)
+        with phase(f"home_{k}{c}"):
+            load_home(k, c, 0).start()
+            for d in OTHERS:
+                back_two(k, c, d).wait()
+                load_home(k, c, d).start()
+        with phase(f"load_{k}{c}"):
+            for d in range(SIDE):
+                load_home(k, c, d).wait()
+        with phase(f"combine_{k}{c}"):
+            combine(k, c)
+
+    def errands(act, whens):
+        out = []
+        for c, when in zip(PARTS, whens):
+
+            def errand(c=c):
+                with phase(f"{act.__name__}_{c}"):
+                    act(c)
+
+            out.append((when, errand))
+        return out
+
+    def forward(c):
+        relay_two(1, c)
+
+    def forward_back(c):
+        relay_back(0, c)
+
+    with phase("wait_rows_0"):
+        wait_rows(0)
+    expert(0, errands(forward, FIRST))
     send_back(0)
-    wait_rows(1)
-    expert(1, during_second)
+    with phase("wait_rows_1"):
+        wait_rows(1)
+    expert(1, errands(forward_back, SECOND))
     send_back(1)
     for c in PARTS:
         bring_home(0, c)
-    for c in PARTS:
-        relay_back(1, c)
+    with phase("weigh_1"):
+        for c in ORDERS:
+            weigh(1, c)
+    for c in PARTS:
+        with phase(f"relay_back_1{c}"):
+            relay_back(1, c)
     for c in PARTS:
         bring_home(1, c)
         for d in OTHERS:
@@ -295,8 +357,9 @@
         span = pl.ds(offset[c], cols[c])
         axis = AXES[c][0]
         total = acc[pl.ds(pl.multiple_of(at[axis] * tokens, tokens), tokens), span]
-        for d in OTHERS:
-            end(c, d).wait()
+        with phase(f"end_{c}"):
+            for d in OTHERS:
+                end(c, d).wait()
         for d in OTHERS:
             total += sums[c][other(axis, d)].astype(F32)
         y_ref[:, span] = total.astype(y_ref.dtype)
@@ -304,14 +367,14 @@
 
 def moe(meta, x, w_gate, w_up, w_down, slots):
     (tokens, depth), inner = x.shape, w_gate.shape[2]
-    third = depth // 128 // 3 * 128
-    cols = (third, third, depth - 2 * third)
+    lanes, more = divmod(depth // 128, len(PARTS))
+    cols = tuple(128 * (lanes + (c in (0, 1, 4, 5, 2, 3)[:more])) for c in PARTS)
     width = min(WIDTH, inner // 2)
     plane = SIDE * SIDE * slots
     box = lambda c, *lead: (*lead, SIDE, SIDE, SIDE, slots // GROUP, GROUP, cols[c])
     hbm = [jax.ShapeDtypeStruct(box(c, 2), BF16) for _ in range(3) for c in PARTS]
     dma = pltpu.SemaphoreType.DMA
-    n = SIDE - 1
+    n, p = SIDE - 1, len(PARTS)
     out = pl.pallas_call(
         functools.partial(kernel, slots, cols, width),
         in_specs=[pl.BlockSpec(memory_space=pltpu.VMEM)] * 2 + [pl.BlockSpec(memory_space=pl.ANY)] * 3,
@@ -323,16 +386,18 @@
         + [pltpu.VMEM((SIDE, tokens, cols[c]), BF16) for c in PARTS]
         + [
             pltpu.VMEM((3, SIDE, *meta.shape), F32),
+            pltpu.VMEM((3, SIDE, plane, tokens), BF16),
             pltpu.VMEM((SIDE * plane, depth), BF16),
             pltpu.VMEM((SIDE * plane, depth), F32),
             pltpu.VMEM((2, depth, width), BF16),
             pltpu.VMEM((2, depth, width), BF16),
             pltpu.VMEM((2, width, depth), BF16),
         ]
-        + [dma((3, n))] * 4
-        + [dma((2, 3, n))] * 8
         + [dma((3, n))] * 2
-        + [dma((3 + SIDE, 2, 3)), dma((2, 3))],
+        + [dma((p, n))] * 2
+        + [dma((2, p, n))] * 8
+        + [dma((p, n))] * 2
+        + [dma((3 + SIDE, 2, p)), dma((2, 3))],
         compiler_params=pltpu.CompilerParams(
             collective_id=0, has_side_effects=True, vmem_limit_bytes=67043328
         ),

time: 241 us -> 203 us (0.84)
  Pallas kernels: 236 us -> 198 us
    pallas_call x1, Pallas kernels: 236 us -> 198 us  [moe(): pl.pallas_call(functools.partial(kernel, slots, cols, width), in_specs=[p...]
where the time goes in v3:
time: 203 us
  Pallas kernels  198 us (98%)
  local copies, waits for them, and re-layouts  2.3 us (1%)
    pallas_call x1, Pallas kernels, moe(): pl.pallas_call(functools.partial(kernel, slots, cols, width), in_specs=[p...  198 us

profile of v3, /device:TPU:0, one launch (start us, length us, event | category | flops | bytes accessed | tf_op | source)
XLA Modules:
  0.0 202.6 jit_solution(11774025140785871041)
XLA Ops:
  0.0 0.7 convert_bitcast_fusion
  0.7 1.3 pad_maximum_fusion.meta_ref
  2.0 198.2 %moe.1 = (bf16[256,2048]{1,0:T(8,128)(2,1)}, bf16[2,4,4,4,5,4,384]{6,5,4,3,2,1,0:T(4,128)(2,1)}, bf16[2,4,4,4,5,4,384]{6,5,4,3,2,1,0:T(4,128)(2,1)}, bf16[2,4,4,...) custom-call(f32[16,256]{1,0:T(8,128)} %pad_maximum_fusion.meta_ref, ...), custom_call_target="tpu_custom_call" | custom-call | tf_op jit(solution)/shard_map/moe/pallas_call | solution.py:378
  200.3 2.3 %copy.9 = bf16[1,1,256,2048]{3,2,1,0:T(8,128)(2,1)} copy(bf16[1,1,256,2048]{3,2,1,0:T(8,128)(2,1)} %bitcast.10) | data formatting | bytes 2097152

commit v4 on v3

--- a/solution.py
+++ b/solution.py
@@ -16,7 +16,8 @@
 GROUP = 4
 WIDTH = 512
 PARTS, ORDERS, OTHERS = range(6), range(3), range(1, SIDE)
-FIRST, SECOND = (4, 4, 5, 5, 6, 7), (2, 3, 4, 5, 6, 7)
+FIRST, SECOND = (2, 2, 3, 5, 5, 6), (2, 3, 4, 5, 7, 7)
+WIDE = (0, 1, 2, 4, 3, 5)
 
 
 def phase(name):
@@ -31,16 +32,17 @@
     return jnp.dot(a, b, preferred_element_type=F32)
 
 
-def kernel(slots, cols, width, meta_ref, x_ref, gate_hbm, up_hbm, down_hbm, y_ref, *rest):
+def kernel(slots, cols, width, expert_hbm, slot_hbm, score_hbm, x_hbm, gate_hbm, up_hbm, down_hbm, y_hbm, *rest):
     rest = list(rest)
     take = lambda n: [rest.pop(0) for _ in range(n)]
     relay, back, home, spread, boxes, rows, sums = (take(len(PARTS)) for _ in range(7))
-    metas, mask, flat, acc, gate_w, up_w, down_w = take(7)
-    bell_s, bell_r, tok_s, tok_r, two_s, two_r, three_s, three_r = take(8)
-    b3_s, b3_r, b2_s, b2_r, end_s, end_r, own, w_sem = take(8)
-
-    tokens, depth = x_ref.shape
-    top = meta_ref.shape[0] // 2
+    expert_v, slot_v, score_v, meta, metas, mask, flat, acc, gate_w, up_w, down_w = take(11)
+    bell_s, bell_r, tok_s, tok_r, pass_s, pass_r, two_s, two_r, three_s, three_r = take(10)
+    b3_s, b3_r, b2_s, b2_r, end_s, end_r, own, w_sem, x_sem, arg_sem = take(10)
+    y_v, y_sem = take(2)
+
+    tokens, depth = x_hbm.shape
+    top = expert_v.shape[0]
     inner = gate_hbm.shape[2]
     steps = inner // width
     plane = SIDE * SIDE * slots
@@ -69,38 +71,54 @@
 
 
     def bell(c, d):
-        return remote(meta_ref, metas.at[c, at[AXES[c][0]]], bell_s.at[c, d - 1], bell_r.at[c, d - 1], AXES[c][0], d)
+        return remote(meta, metas.at[c, at[AXES[c][0]]], bell_s.at[c], bell_r.at[c], AXES[c][0], d)
+
+    def token_own(c):
+        return pltpu.make_async_copy(
+            x_hbm.at[:, pl.ds(offset[c], cols[c])], spread[c].at[at[AXES[c][0]]], x_sem
+        )
 
     def token(c, d):
-        src = x_ref.at[:, pl.ds(offset[c], cols[c])]
-        return remote(src, spread[c].at[at[AXES[c][0]]], tok_s.at[c, d - 1], tok_r.at[c, d - 1], AXES[c][0], d)
+        mine = spread[c].at[at[AXES[c][0]]]
+        return remote(mine, mine, tok_s.at[c], tok_r.at[c], AXES[c][0], d)
+
+    def forward_token(c, d):
+        half = tokens // 2
+        theirs = spread[c].at[other(AXES[c][0], SIDE - d), pl.ds(d // 2 * half, half)]
+        return remote(theirs, theirs, pass_s.at[c], pass_r.at[c], AXES[c][0], d)
 
     def two(k, c, d):
         axis = AXES[c][1]
         src, dst = boxes[c].at[other(axis, d)], second(relay[c].at[k], c, at[axis])
-        return remote(src, dst, two_s.at[k, c, d - 1], two_r.at[k, c, d - 1], axis, d)
+        return remote(src, dst, two_s.at[c], two_r.at[k, c], axis, d)
+
+    def piece(c, e, d):
+        axis, s = AXES[c][1], other(AXES[c][0], e)
+        src = boxes[c].at[other(axis, d), s]
+        dst = relay[c].at[0, at[axis], s] if c % 3 == 2 else relay[c].at[0, s, at[axis]]
+        return remote(src, dst, two_s.at[c], two_r.at[0, c], axis, d)
 
     def two_own(k, c):
         p = at[AXES[c][1]]
-        return pltpu.make_async_copy(boxes[c].at[p], second(relay[c].at[k], c, p), own.at[0, k, c])
+        return pltpu.make_async_copy(boxes[c].at[p], second(relay[c].at[k], c, p), own.at[0, c])
 
     def three(k, c, d):
         axis = AXES[c][2]
         src, dst = relay[c].at[k, :, :, other(axis, d)], third(rows[c].at[k], c, at[axis])
-        return remote(src, dst, three_s.at[k, c, d - 1], three_r.at[k, c, d - 1], axis, d)
+        return remote(src, dst, three_s.at[c], three_r.at[k, c], axis, d)
 
     def three_own(k, c):
         p = at[AXES[c][2]]
-        return pltpu.make_async_copy(relay[c].at[k, :, :, p], third(rows[c].at[k], c, p), own.at[1, k, c])
+        return pltpu.make_async_copy(relay[c].at[k, :, :, p], third(rows[c].at[k], c, p), own.at[1, c])
 
     def back_three(k, c, d):
         axis = AXES[c][2]
         src, dst = third(rows[c].at[k], c, other(axis, d)), back[c].at[k, at[axis]]
-        return remote(src, dst, b3_s.at[k, c, d - 1], b3_r.at[k, c, d - 1], axis, d)
+        return remote(src, dst, b3_s.at[c], b3_r.at[k, c], axis, d)
 
     def back_three_own(k, c):
         p = at[AXES[c][2]]
-        return pltpu.make_async_copy(third(rows[c].at[k], c, p), back[c].at[k, p], own.at[2, k, c])
+        return pltpu.make_async_copy(third(rows[c].at[k], c, p), back[c].at[k, p], own.at[2, c])
 
     def returned(k, c, p):
         return back[c].at[k, :, p] if c % 3 == 2 else back[c].at[k, :, :, p]
@@ -108,17 +126,17 @@
     def back_two(k, c, d):
         axis = AXES[c][1]
         src, dst = returned(k, c, other(axis, d)), home[c].at[k, at[axis]]
-        return remote(src, dst, b2_s.at[k, c, d - 1], b2_r.at[k, c, d - 1], axis, d)
+        return remote(src, dst, b2_s.at[c], b2_r.at[k, c], axis, d)
 
     def load_home(k, c, d):
         p = other(AXES[c][1], SIDE - d)
         src = returned(k, c, p) if d == 0 else home[c].at[k, p]
-        return pltpu.make_async_copy(src, boxes[c].at[p], own.at[3 + d, k, c])
+        return pltpu.make_async_copy(src, boxes[c].at[p], own.at[3, c])
 
     def end(c, d):
         axis = AXES[c][0]
         src, dst = spread[c].at[other(axis, d)], sums[c].at[at[axis]]
-        return remote(src, dst, end_s.at[c, d - 1], end_r.at[c, d - 1], axis, d)
+        return remote(src, dst, end_s.at[c], end_r.at[c], axis, d)
 
     def weights(n):
         k, cut, s = n // steps, pl.ds(lax.rem(n, steps) * width, width), lax.rem(n, 2)
@@ -128,6 +146,13 @@
             pltpu.make_async_copy(down_hbm.at[k, cut, :], down_w.at[s], w_sem.at[s, 2]),
         )
 
+    def drain(ref, *sems):
+        for sem in sems:
+            pltpu.make_async_copy(ref, ref, sem).wait()
+
+    def blocks(c, n=SIDE - 1):
+        return boxes[c].at[pl.ds(0, n)]
+
 
     def place_of_row(k, c):
         r = iota((plane, tokens), 0)
@@ -135,14 +160,17 @@
         device = at[a1] * stride[a1] + r // (SIDE * slots) * stride[a2] + r // slots % SIDE * stride[a3]
         return ((2 * device + k) * slots + r % slots).astype(F32)
 
+    def choose_from(k, c, s, place):
+        hit = place == metas[c, s, 0:1, :]
+        for j in range(1, top):
+            hit = hit | (place == metas[c, s, j : j + 1, :])
+        mask[c, s] = jnp.where(hit, 1.0, 0.0).astype(BF16)
+
     def choose(k, c):
         place = place_of_row(k, c)
 
         def one(s, carry):
-            hit = place == metas[c, s, 0:1, :]
-            for j in range(1, top):
-                hit = hit | (place == metas[c, s, j : j + 1, :])
-            mask[c, s] = jnp.where(hit, 1.0, 0.0).astype(BF16)
+            choose_from(k, c, s, place)
             return carry
 
         lax.fori_loop(0, SIDE, one, 0)
@@ -160,10 +188,13 @@
 
         lax.fori_loop(0, SIDE, one, 0)
 
+    def pack_from(c, s):
+        out = dot(mask[c % 3, s], spread[c][s]).astype(BF16)
+        boxes[c][:, s] = out.reshape(SIDE, SIDE, slots // GROUP, GROUP, cols[c])
+
     def pack(c):
         def one(s, carry):
-            out = dot(mask[c % 3, s], spread[c][s]).astype(BF16)
-            boxes[c][:, s] = out.reshape(SIDE, SIDE, slots // GROUP, GROUP, cols[c])
+            pack_from(c, s)
             return carry
 
         lax.fori_loop(0, SIDE, one, 0)
@@ -231,26 +262,38 @@
         for d in OTHERS:
             target = me + (other(axis, d) - at[axis]) * stride[axis]
             pl.semaphore_signal(barrier, inc=1, device_id=(dp, target), device_id_type=MESH)
-    for copy in weights(0):
+    arguments = [
+        pltpu.make_async_copy(src, dst, arg_sem.at[i])
+        for i, (src, dst) in enumerate(((expert_hbm, expert_v), (slot_hbm, slot_v), (score_hbm, score_v)))
+    ]
+    for copy in arguments:
         copy.start()
+    for c in PARTS:
+        token_own(c).start()
+    for copy in arguments:
+        copy.wait()
+    slot = slot_v[...]
+    meta[0:top, :] = jnp.where(slot < slots, expert_v[...] * slots + slot, -1).astype(F32)
+    meta[top:, :] = score_v[...]
     for c in ORDERS:
-        metas[c, at[AXES[c][0]]] = meta_ref[...]
-    for c in PARTS:
-        spread[c][at[AXES[c][0]]] = x_ref[:, pl.ds(offset[c], cols[c])]
+        metas[c, at[AXES[c][0]]] = meta[...]
+    drain(x_hbm, x_sem)
     with phase("barrier"):
         pl.semaphore_wait(barrier, 3 * (SIDE - 1))
 
+    NEAR = (1, SIDE - 1)
     for d in OTHERS:
         for c in ORDERS:
             bell(c, d).start()
     for c in PARTS:
-        for d in OTHERS:
+        for d in NEAR:
             token(c, d).start()
+    for copy in weights(0):
+        copy.start()
 
     def relay_two(k, c):
         two_own(k, c).wait()
-        for d in OTHERS:
-            two(k, c, d).wait()
+        drain(blocks(c), two_s.at[c], two_r.at[k, c])
         for d in OTHERS:
             three(k, c, d).start()
         three_own(k, c).start()
@@ -261,17 +304,52 @@
             two(k, c, d).start()
         two_own(k, c).start()
 
-    for c in ORDERS:
-        with phase(f"choose_0{c}"):
-            for d in OTHERS:
-                bell(c, d).wait()
-            choose(0, c)
+    def forward_tokens(c):
+        drain(spread[c].at[pl.ds(0, 2)], tok_s.at[c], tok_r.at[c])
+        for d in NEAR:
+            forward_token(c, d).start()
+
+    def send_pieces(c, e):
+        pack_from(c, other(AXES[c][0], e))
+        for d in OTHERS:
+            piece(c, e, d).start()
+
+    def send_near(c):
+        def one(i, carry):
+            send_pieces(c, 1 + 2 * i)
+            return carry
+
+        lax.fori_loop(0, 2, one, 0)
+
+    for o in ORDERS:
+        with phase(f"own_{o}"):
+            choose_from(0, o, at[AXES[o][0]], place_of_row(0, o))
+            for c in PARTS[o::3]:
+                send_pieces(c, 0)
+    for c in PARTS:
+        with phase(f"pass_{c}"):
+            forward_tokens(c)
+        if c == 2:
+            for o in ORDERS:
+                with phase(f"choose_0{o}"):
+                    drain(metas.at[o, pl.ds(0, SIDE - 1)], bell_s.at[o], bell_r.at[o])
+                    place = place_of_row(0, o)
+
+                    def one(e, carry, o=o, place=place):
+                        choose_from(0, o, other(AXES[o][0], e), place)
+                        return carry
+
+                    lax.fori_loop(1, SIDE, one, 0)
+        if c % 3 == 2:
+            for n in range(c - 2, c + 1):
+                with phase(f"near_{n}"):
+                    send_near(n)
     for c in PARTS:
         with phase(f"spread_wait_{c}"):
-            for d in OTHERS:
-                token(c, d).wait()
+            drain(spread[c].at[0], pass_s.at[c], pass_r.at[c])
         with phase(f"pack_0{c}"):
-            send_boxes(0, c)
+            send_pieces(c, 2)
+            two_own(0, c).start()
     with phase("choose_1"):
         for c in ORDERS:
             choose(1, c)
@@ -287,8 +365,7 @@
 
     def wait_rows(k):
         for c in PARTS:
-            for d in OTHERS:
-                three(k, c, d).wait()
+            drain(blocks(c), three_s.at[c], three_r.at[k, c])
             three_own(k, c).wait()
 
     def send_back(k):
@@ -299,20 +376,20 @@
 
     def relay_back(k, c):
         back_three_own(k, c).wait()
-        for d in OTHERS:
-            back_three(k, c, d).wait()
+        drain(blocks(c), b3_s.at[c], b3_r.at[k, c])
         for d in OTHERS:
             back_two(k, c, d).start()
 
     def bring_home(k, c):
         with phase(f"home_{k}{c}"):
             load_home(k, c, 0).start()
+            drain(blocks(c), b2_s.at[c], b2_r.at[k, c])
             for d in OTHERS:
-                back_two(k, c, d).wait()
                 load_home(k, c, d).start()
+
+    def sum_up(k, c):
         with phase(f"load_{k}{c}"):
-            for d in range(SIDE):
-                load_home(k, c, d).wait()
+            drain(blocks(c, SIDE), own.at[3, c])
         with phase(f"combine_{k}{c}"):
             combine(k, c)
 
@@ -343,49 +420,65 @@
     send_back(1)
     for c in PARTS:
         bring_home(0, c)
+        if c % 3 == 2:
+            for n in range(c - 2, c + 1):
+                sum_up(0, n)
     with phase("weigh_1"):
         for c in ORDERS:
             weigh(1, c)
     for c in PARTS:
         with phase(f"relay_back_1{c}"):
             relay_back(1, c)
+    def finish(c):
+        sum_up(1, c)
+        for d in OTHERS:
+            end(c, d).start()
+
     for c in PARTS:
         bring_home(1, c)
-        for d in OTHERS:
-            end(c, d).start()
+        if c % 3:
+            finish(c - 1)
+        if c % 3 == 2:
+            finish(c)
     for c in PARTS:
         span = pl.ds(offset[c], cols[c])
         axis = AXES[c][0]
         total = acc[pl.ds(pl.multiple_of(at[axis] * tokens, tokens), tokens), span]
         with phase(f"end_{c}"):
-            for d in OTHERS:
-                end(c, d).wait()
+            drain(sums[c].at[pl.ds(0, SIDE - 1)], end_s.at[c], end_r.at[c])
         for d in OTHERS:
             total += sums[c][other(axis, d)].astype(F32)
-        y_ref[:, span] = total.astype(y_ref.dtype)
-
-
-def moe(meta, x, w_gate, w_up, w_down, slots):
+        y_v[:, span] = total.astype(y_v.dtype)
+        pltpu.make_async_copy(y_v.at[:, span], y_hbm.at[:, span], y_sem).start()
+    with phase("result"):
+        drain(y_v, y_sem)
+
+
+def moe(expert, slot, gate, x, w_gate, w_up, w_down, slots):
     (tokens, depth), inner = x.shape, w_gate.shape[2]
     lanes, more = divmod(depth // 128, len(PARTS))
-    cols = tuple(128 * (lanes + (c in (0, 1, 4, 5, 2, 3)[:more])) for c in PARTS)
+    cols = tuple(128 * (lanes + (c in WIDE[:more])) for c in PARTS)
     width = min(WIDTH, inner // 2)
     plane = SIDE * SIDE * slots
     box = lambda c, *lead: (*lead, SIDE, SIDE, SIDE, slots // GROUP, GROUP, cols[c])
     hbm = [jax.ShapeDtypeStruct(box(c, 2), BF16) for _ in range(3) for c in PARTS]
     dma = pltpu.SemaphoreType.DMA
-    n, p = SIDE - 1, len(PARTS)
+    p = len(PARTS)
     out = pl.pallas_call(
         functools.partial(kernel, slots, cols, width),
-        in_specs=[pl.BlockSpec(memory_space=pltpu.VMEM)] * 2 + [pl.BlockSpec(memory_space=pl.ANY)] * 3,
-        out_specs=[pl.BlockSpec(memory_space=pltpu.VMEM)] + [pl.BlockSpec(memory_space=pl.ANY)] * len(hbm),
+        in_specs=[pl.BlockSpec(memory_space=pl.ANY)] * 7,
+        out_specs=[pl.BlockSpec(memory_space=pl.ANY)] * (1 + len(hbm)),
         out_shape=[jax.ShapeDtypeStruct((tokens, depth), BF16)] + hbm,
         scratch_shapes=[pltpu.VMEM((SIDE, tokens, cols[c]), BF16) for c in PARTS]
         + [pltpu.VMEM(box(c), BF16) for c in PARTS]
         + [pltpu.VMEM(box(c, 2), BF16) for c in PARTS]
         + [pltpu.VMEM((SIDE, tokens, cols[c]), BF16) for c in PARTS]
         + [
-            pltpu.VMEM((3, SIDE, *meta.shape), F32),
+            pltpu.VMEM(expert.shape, I32),
+            pltpu.VMEM(slot.shape, I32),
+            pltpu.VMEM(gate.shape, F32),
+            pltpu.VMEM((2 * expert.shape[0], tokens), F32),
+            pltpu.VMEM((3, SIDE, 2 * expert.shape[0], tokens), F32),
             pltpu.VMEM((3, SIDE, plane, tokens), BF16),
             pltpu.VMEM((SIDE * plane, depth), BF16),
             pltpu.VMEM((SIDE * plane, depth), F32),
@@ -393,16 +486,17 @@
             pltpu.VMEM((2, depth, width), BF16),
             pltpu.VMEM((2, width, depth), BF16),
         ]
-        + [dma((3, n))] * 2
-        + [dma((p, n))] * 2
-        + [dma((2, p, n))] * 8
-        + [dma((p, n))] * 2
-        + [dma((3 + SIDE, 2, p)), dma((2, 3))],
+        + [dma((3,))] * 2
+        + [dma((p,))] * 4
+        + [dma((p,)), dma((2, p))] * 4
+        + [dma((p,))] * 2
+        + [dma((4, p)), dma((2, 3)), dma, dma((3,))]
+        + [pltpu.VMEM((tokens, depth), BF16), dma],
         compiler_params=pltpu.CompilerParams(
             collective_id=0, has_side_effects=True, vmem_limit_bytes=67043328
         ),
         name="moe",
-    )(meta, x, w_gate, w_up, w_down)
+    )(expert, slot, gate, x, w_gate, w_up, w_down)
     return out[0]
 
 
@@ -413,9 +507,7 @@
         tokens = x.shape[2]
         slots = 5 * tokens * expert.shape[3] // (4 * 2 * members)
         x, expert, slot, gate = x[0, 0], expert[0, 0], slot[0, 0], gate[0, 0]
-        place = jnp.where(slot < slots, expert * slots + slot, -1)
-        meta = jnp.concatenate([place.astype(F32).T, gate.T])
-        return moe(meta, x, w_gate, w_up, w_down, slots)[None, None]
+        return moe(expert.T, slot.T, gate.T, x, w_gate, w_up, w_down, slots)[None, None]
 
     spread, held = P("dp", "ep"), P("ep")
     return jax.shard_map(

time: 203 us -> 194 us (0.956)
  Pallas kernels: 198 us -> 192 us
    pallas_call x1, Pallas kernels: 198 us -> 192 us  [moe(): pl.pallas_call(functools.partial(kernel, slots, cols, width), in_specs=[p...]
where the time goes in v4:
time: 194 us
  Pallas kernels  192 us (99%)
  local copies, waits for them, and re-layouts  2.3 us (1%)
    pallas_call x1, Pallas kernels, moe(): pl.pallas_call(functools.partial(kernel, slots, cols, width), in_specs=[p...  192 us

profile of v4, /device:TPU:0, one launch (start us, length us, event | category | flops | bytes accessed | tf_op | source)
XLA Modules:
  0.0 194.2 jit_solution(14156717604189782030)
XLA Ops:
  0.0 191.9 %moe.1 = (bf16[256,2048]{1,0:T(8,128)(2,1)}, bf16[2,4,4,4,5,4,384]{6,5,4,3,2,1,0:T(4,128)(2,1)}, bf16[2,4,4,4,5,4,384]{6,5,4,3,2,1,0:T(4,128)(2,1)}, bf16[2,4,4,...) custom-call(s32[8,256]{1,0:T(8,128)} %bitcast.13, ...), custom_call_target="tpu_custom_call" | custom-call | tf_op jit(solution)/shard_map/moe/pallas_call | solution.py:467
  191.9 2.3 %copy.9 = bf16[1,1,256,2048]{3,2,1,0:T(8,128)(2,1)} copy(bf16[1,1,256,2048]{3,2,1,0:T(8,128)(2,1)} %bitcast.12) | data formatting | bytes 2097152

commit v5 on v4

--- a/solution.py
+++ b/solution.py
@@ -13,10 +13,11 @@
 SIDE = 4
 STRIDE = (SIDE * SIDE, SIDE, 1)
 AXES = ((0, 1, 2), (1, 2, 0), (2, 0, 1)) * 2
+BACK = tuple((c + 2) % 3 for c in range(6))
 GROUP = 4
 WIDTH = 512
 PARTS, ORDERS, OTHERS = range(6), range(3), range(1, SIDE)
-FIRST, SECOND = (2, 2, 3, 5, 5, 6), (2, 3, 4, 5, 7, 7)
+FIRST, SECOND = (2, 2, 3, 5, 5, 6), (4, 5, 5, 6, 7, 8)
 WIDE = (0, 1, 2, 4, 3, 5)
 
 
@@ -63,11 +64,11 @@
         )
 
 
-    def third(ref, c, p):
-        return (ref.at[:, :, p], ref.at[p], ref.at[:, p])[c % 3]
-
-    def second(ref, c, p):
-        return ref.at[p] if c % 3 == 2 else ref.at[:, p]
+    def third(ref, o, p):
+        return (ref.at[:, :, p], ref.at[p], ref.at[:, p])[o % 3]
+
+    def second(ref, o, p):
+        return ref.at[p] if o % 3 == 2 else ref.at[:, p]
 
 
     def bell(c, d):
@@ -112,29 +113,29 @@
         return pltpu.make_async_copy(relay[c].at[k, :, :, p], third(rows[c].at[k], c, p), own.at[1, c])
 
     def back_three(k, c, d):
-        axis = AXES[c][2]
-        src, dst = third(rows[c].at[k], c, other(axis, d)), back[c].at[k, at[axis]]
+        axis = AXES[BACK[c]][2]
+        src, dst = third(rows[c].at[k], BACK[c], other(axis, d)), back[c].at[k, at[axis]]
         return remote(src, dst, b3_s.at[c], b3_r.at[k, c], axis, d)
 
     def back_three_own(k, c):
-        p = at[AXES[c][2]]
-        return pltpu.make_async_copy(third(rows[c].at[k], c, p), back[c].at[k, p], own.at[2, c])
+        p = at[AXES[BACK[c]][2]]
+        return pltpu.make_async_copy(third(rows[c].at[k], BACK[c], p), back[c].at[k, p], own.at[2, c])
 
     def returned(k, c, p):
-        return back[c].at[k, :, p] if c % 3 == 2 else back[c].at[k, :, :, p]
+        return back[c].at[k, :, p] if BACK[c] == 2 else back[c].at[k, :, :, p]
 
     def back_two(k, c, d):
-        axis = AXES[c][1]
+        axis = AXES[BACK[c]][1]
         src, dst = returned(k, c, other(axis, d)), home[c].at[k, at[axis]]
         return remote(src, dst, b2_s.at[c], b2_r.at[k, c], axis, d)
 
     def load_home(k, c, d):
-        p = other(AXES[c][1], SIDE - d)
+        p = other(AXES[BACK[c]][1], SIDE - d)
         src = returned(k, c, p) if d == 0 else home[c].at[k, p]
         return pltpu.make_async_copy(src, boxes[c].at[p], own.at[3, c])
 
     def end(c, d):
-        axis = AXES[c][0]
+        axis = AXES[BACK[c]][0]
         src, dst = spread[c].at[other(axis, d)], sums[c].at[at[axis]]
         return remote(src, dst, end_s.at[c], end_r.at[c], axis, d)
 
@@ -204,7 +205,7 @@
 
         def one(s, carry):
             got = boxes[c][:, :, s].reshape(plane, cols[c])
-            part = lax.dot_general(mask[c % 3, s], got, (((0,), (0,)), ((), ())), preferred_element_type=F32)
+            part = lax.dot_general(mask[BACK[c], s], got, (((0,), (0,)), ((), ())), preferred_element_type=F32)
             r = pl.ds(pl.multiple_of(s * tokens, tokens), tokens)
             if k == 0:
                 acc[r, span] = part
@@ -442,7 +443,7 @@
             finish(c)
     for c in PARTS:
         span = pl.ds(offset[c], cols[c])
-        axis = AXES[c][0]
+        axis = AXES[BACK[c]][0]
         total = acc[pl.ds(pl.multiple_of(at[axis] * tokens, tokens), tokens), span]
         with phase(f"end_{c}"):
             drain(sums[c].at[pl.ds(0, SIDE - 1)], end_s.at[c], end_r.at[c])

time: 194 us -> 193 us (level)
  Pallas kernels: 192 us -> 190 us
    pallas_call x1, Pallas kernels: 192 us -> 190 us  [moe(): pl.pallas_call(functools.partial(kernel, slots, cols, width), in_specs=[p...]
where the time goes in v5:
time: 193 us; the launch traced here: 192 us
  Pallas kernels  190 us (98%)
  local copies, waits for them, and re-layouts  2.3 us (1%)
    pallas_call x1, Pallas kernels, moe(): pl.pallas_call(functools.partial(kernel, slots, cols, width), in_specs=[p...  190 us

profile of v5, /device:TPU:0, one launch (start us, length us, event | category | flops | bytes accessed | tf_op | source)
XLA Modules:
  0.0 192.0 jit_solution(5134260154633249880)
XLA Ops:
  0.0 189.7 %moe.1 = (bf16[256,2048]{1,0:T(8,128)(2,1)}, bf16[2,4,4,4,5,4,384]{6,5,4,3,2,1,0:T(4,128)(2,1)}, bf16[2,4,4,4,5,4,384]{6,5,4,3,2,1,0:T(4,128)(2,1)}, bf16[2,4,4,...) custom-call(s32[8,256]{1,0:T(8,128)} %bitcast.13, ...), custom_call_target="tpu_custom_call" | custom-call | tf_op jit(solution)/shard_map/moe/pallas_call | solution.py:468
  189.7 2.3 %copy.9 = bf16[1,1,256,2048]{3,2,1,0:T(8,128)(2,1)} copy(bf16[1,1,256,2048]{3,2,1,0:T(8,128)(2,1)} %bitcast.12) | data formatting | bytes 2097152

commit v6 on v5

--- a/solution.py
+++ b/solution.py
@@ -12,13 +12,13 @@
 MESH = pl.DeviceIdType.MESH
 SIDE = 4
 STRIDE = (SIDE * SIDE, SIDE, 1)
-AXES = ((0, 1, 2), (1, 2, 0), (2, 0, 1)) * 2
-BACK = tuple((c + 2) % 3 for c in range(6))
+AXES = ((0, 1, 2), (1, 2, 0), (2, 0, 1)) * 3
+BACK = tuple((c + 2) % 3 for c in range(9))
 GROUP = 4
 WIDTH = 512
-PARTS, ORDERS, OTHERS = range(6), range(3), range(1, SIDE)
-FIRST, SECOND = (2, 2, 3, 5, 5, 6), (4, 5, 5, 6, 7, 8)
-WIDE = (0, 1, 2, 4, 3, 5)
+PARTS, ORDERS, OTHERS = range(9), range(3), range(1, SIDE)
+FIRST, SECOND = (2, 2, 3, 4, 4, 5, 6, 6, 6), (4, 4, 5, 5, 6, 6, 7, 8, 8)
+WIDE = (0, 1, 2, 3, 4, 5, 7, 6, 8)
 
 
 def phase(name):

time: 193 us -> 193 us (level)
  no operation moved by 1% of the time
where the time goes in v6:
time: 193 us; the launch traced here: 192 us
  Pallas kernels  190 us (98%)
  local copies, waits for them, and re-layouts  2.3 us (1%)
    pallas_call x1, Pallas kernels, moe(): pl.pallas_call(functools.partial(kernel, slots, cols, width), in_specs=[p...  190 us

profile of v6, /device:TPU:0, one launch (start us, length us, event | category | flops | bytes accessed | tf_op | source)
XLA Modules:
  0.0 192.4 jit_solution(4898105334603630964)
XLA Ops:
  0.0 190.1 %moe.1 = (bf16[256,2048]{1,0:T(8,128)(2,1)}, bf16[2,4,4,4,5,4,256]{6,5,4,3,2,1,0:T(4,128)(2,1)}, bf16[2,4,4,4,5,4,256]{6,5,4,3,2,1,0:T(4,128)(2,1)}, bf16[2,4,4,...) custom-call(s32[8,256]{1,0:T(8,128)} %bitcast.13, ...), custom_call_target="tpu_custom_call" | custom-call | tf_op jit(solution)/shard_map/moe/pallas_call | solution.py:468
  190.1 2.3 %copy.9 = bf16[1,1,256,2048]{3,2,1,0:T(8,128)(2,1)} copy(bf16[1,1,256,2048]{3,2,1,0:T(8,128)(2,1)} %bitcast.12) | data formatting | bytes 2097152
